TPU v7x, 512 devices: a whole 4x8x8 slice. The times are simulated.
512 devices in a mesh: member: 32 (over x, z), tile: 16 (over y, core).
Axes of the slice: x: 4, y: 8, z: 8, core: 2. Of those that a mesh axis runs over, the one named last changes fastest.
Arguments:
- ensemble: bfloat16 [256, 2048, 320], P('member', 'tile'), may hold values from -6 to 6
- departures: bfloat16 [2048, 128, 256], P(('tile', 'member')), may hold values from -6 to 6
- innovations: float32 [2048, 128], P(('tile', 'member')), may hold values from -12 to 12
- precision: float32 [2048, 128], P(('tile', 'member')), may hold values from 0.2 to 5
- obs_count: int32 [2048], P(('tile', 'member')), may hold values from 16 to 128
- tile_counts: int32 [16], replicated, may hold values from 0 to 128, as said below
Outputs:
- analysis: bfloat16 [256, 2048, 320], P('member', 'tile')
Inputs may be any that keep to these rules, and one draw needn't show every extreme that they name: `tile_counts`: each count is a multiple of 32; all counts sum to 1024, and for every tile t the counts of tiles 0 to t - 1 sum to t * 32 * 2 plus or minus at most 32.
All inputs are finite; a program needn't handle non-finite values.
Results may differ from a plain program's by a relative error of at most 0.0049.
Values may be sent and summed in bfloat16 or wider, within the bound.
No kernel may reach another device: no remote copies, remote signals or barrier semaphores. Data moves between devices by JAX's collectives and lax.ppermute only.
A program may use at most 64 MiB of HBM per device.

v0:
```python
import jax
import jax.numpy as jnp
from jax import lax
from jax.experimental import pallas as pl
from jax.experimental.pallas import tpu as pltpu
from jax.sharding import PartitionSpec as P

ITERS = 6
F32 = jnp.float32
BF16 = jnp.bfloat16


def iota(shape, axis):
    return lax.broadcasted_iota(jnp.int32, shape, axis)


def dot(a, b, dims):
    return lax.dot_general(a, b, ((dims[:1], dims[1:]), ((), ())), preferred_element_type=F32)


def pack_kernel(x_ref, out_ref, rows_ref, *, slots, groups):
    part_rows, length, width = x_ref.shape
    capacity = width // groups
    head = (length // 128) * 128
    tail = length - head
    evens, odds = (slots + 1) // 2, slots // 2

    def pick(count, odd):
        shape = (count * groups, width)
        row = iota(shape, 0)
        slot = 2 * (row // groups) + odd
        return (iota(shape, 1) == (row % groups) * capacity + slot).astype(BF16)

    pick_even = pick(evens, 0)
    pick_odd = pick(odds, 1)
    low = iota((groups, 128), 1) < tail
    for m in range(part_rows):
        x = x_ref[m]
        even = dot(pick_even, jnp.concatenate([x, x[: 128 - tail]], axis=0), (1, 1))
        odd = dot(pick_odd, jnp.concatenate([x[head:], x], axis=0), (1, 1))
        here = pl.ds(m, groups, stride=part_rows)
        for p in range(evens):
            base = 2 * p * length
            a = even[p * groups : (p + 1) * groups]
            if p < odds:
                b = odd[p * groups : (p + 1) * groups]
                joined = jnp.concatenate(
                    [a[:, :head], jnp.where(low, a[:, head:], b[:, :128]), b[:, 128:]], axis=1
                )
                for t in range(2 * length // 128):
                    rows_ref[base // 128 + t, here, :] = joined[:, 128 * t : 128 * (t + 1)]
            else:
                for t in range(a.shape[1] // 128):
                    rows_ref[base // 128 + t, here, :] = a[:, 128 * t : 128 * (t + 1)]
    for t in range(rows_ref.shape[0]):
        end = min(128, out_ref.shape[1] - 128 * t)
        out_ref[:, pl.ds(128 * t, end)] = rows_ref[t][:, :end].astype(BF16)


def unpack_kernel(live_ref, x_ref, y_ref, out_ref, rows_ref, *, slots, groups):
    part_rows, length, width = x_ref.shape
    capacity = width // groups
    head = (length // 128) * 128
    tail = length - head
    evens, odds = (slots + 1) // 2, slots // 2

    def place(count, odd):
        shape = (count * groups, width)
        row = iota(shape, 0)
        slot = 2 * (row // groups) + odd
        return (iota(shape, 1) == (row % groups) * capacity + slot).astype(BF16)

    place_even = place(evens, 0)
    place_odd = place(odds, 1)
    for t in range(rows_ref.shape[0]):
        end = min(128, y_ref.shape[1] - 128 * t)
        rows_ref[t, :, pl.ds(0, end)] = y_ref[:, pl.ds(128 * t, end)].astype(F32)
    new = iota((length, width), 1) % capacity < live_ref[0]
    for m in range(part_rows):
        here = pl.ds(m, groups, stride=part_rows)
        parts = []
        for p in range(evens):
            first = 2 * p * length // 128
            tiles = [rows_ref[first + t, here, :] for t in range(head // 128 + 1)]
            parts.append(jnp.concatenate(tiles, axis=1)[:, :length])
        even = jnp.concatenate(parts, axis=0).astype(BF16)
        result = dot(even, place_even, (0, 0))
        parts = []
        for p in range(odds):
            first = (2 * p * length + head) // 128
            tiles = [rows_ref[first + t, here, :] for t in range(head // 128 + 1)]
            parts.append(jnp.concatenate(tiles, axis=1))
        odd = jnp.concatenate(parts, axis=0).astype(BF16)
        result = result + dot(odd, place_odd, (0, 0))[tail:]
        out_ref[m] = jnp.where(new, result, x_ref[m].astype(F32)).astype(BF16)


def split(x):
    high = x.astype(BF16)
    return high, (x - high.astype(F32)).astype(BF16)


def left_of(x):
    high, low = split(x)
    return jnp.concatenate([high, low, high, low], axis=1)


def right_of(x):
    high, low = split(x)
    return jnp.concatenate([high, high, low, low], axis=0)


def total(x):
    return jnp.sum(jnp.sum(x, axis=0, keepdims=True), axis=1, keepdims=True)


def transform_kernel(
    count_ref, dep_ref, inn_ref, prec_ref, out_ref, scaled_ref, h_ref, right_ref, rest_ref, inner_ref
):
    slots, members = out_ref.shape[0], out_ref.shape[1]
    obs = dep_ref.shape[1]
    rank = members - 1.0
    eye = (iota((members, members), 0) == iota((members, members), 1)).astype(F32)
    on_diagonal = iota((obs, obs), 0) == iota((obs, obs), 1)
    eye_obs = on_diagonal.astype(F32)
    f, z, norm_inv, signal = [], [], [], []
    for i in range(slots):
        weight = jnp.where(iota((1, obs), 1) < count_ref[i], jnp.sqrt(prec_ref[i : i + 1, :]), 0.0)
        column = jnp.sum(jnp.where(on_diagonal, weight, 0.0), axis=1, keepdims=True)
        scaled = (dep_ref[i].astype(F32) * column).astype(BF16)
        scaled_ref[i] = scaled
        signal.append((weight * inn_ref[i : i + 1, :]).astype(BF16).astype(F32))
        outer = dot(scaled, scaled, (1, 1))
        squares = total(outer * outer) + (2.0 * rank) * total(outer * eye_obs)
        norm_inv.append(1.0 / jnp.sqrt(squares + members * rank * rank))
        f.append(1.5 - (0.5 * rank) * norm_inv[i])
        z.append(f[i])
        h_ref[i] = outer * norm_inv[i]
    for i in range(slots):
        h = h_ref[i]
        right = right_of(h)
        right_ref[i] = right
        second = 0.25 * h - f[i] * eye_obs
        third = (f[i] * second + (0.5 * f[i]) * h - (0.5 * f[i] * f[i]) * eye_obs) - 0.125 * dot(
            left_of(h), right, (1, 0)
        )
        rest_ref[i] = third - 1.5 * second
        inner_ref[i] = -0.5 * eye_obs
        f[i] = 1.5 - 1.5 * f[i] * f[i] + f[i] * f[i] * f[i]

    def step(_, carried):
        f, z = list(carried[:slots]), list(carried[slots:])
        moved = [left_of(dot(left_of(rest_ref[i]), right_ref[i], (1, 0))) for i in range(slots)]
        seconds = []
        for i in range(slots):
            rest, inner = rest_ref[i], inner_ref[i]
            both = dot(moved[i], right_of(jnp.concatenate([inner, rest], axis=1)), (1, 0))
            inner_ref[i] = f[i] * inner + z[i] * rest + both[:, :obs]
            seconds.append((2.0 * f[i]) * rest + both[:, obs:])
            z[i] = f[i] * z[i]
        for i in range(slots):
            third = dot(moved[i], right_of(seconds[i]), (1, 0))
            third = third + f[i] * seconds[i] + (f[i] * f[i]) * rest_ref[i]
            rest_ref[i] = third - 1.5 * seconds[i]
            f[i] = 1.5 - 1.5 * f[i] * f[i] + f[i] * f[i] * f[i]
        return tuple(f) + tuple(z)

    carried = lax.fori_loop(0, ITERS - 2, step, tuple(f) + tuple(z))
    f, z = carried[:slots], carried[slots:]
    for i in range(slots):
        rest, inner = rest_ref[i], inner_ref[i]
        moved = left_of(dot(left_of(rest), right_ref[i], (1, 0)))
        inner_ref[i] = f[i] * inner + z[i] * rest + dot(moved, right_of(inner), (1, 0))
    for i in range(slots):
        inner, h, scaled = inner_ref[i], h_ref[i], scaled_ref[i]
        scale = f[i] * z[i]
        pull = signal[i]
        for _ in range(2):
            across = jnp.sum(inner * pull, axis=1, keepdims=True)
            pull = scale * pull + jnp.sum(h * across, axis=0, keepdims=True)
        pieces = []
        for _ in range(3):
            pieces.append(pull.astype(BF16).astype(F32))
            pull = pull - pieces[-1]
        pieces.append(jnp.zeros((5, obs), F32))
        rows = dot(jnp.concatenate(pieces, axis=0).astype(BF16), scaled, (1, 0))
        shift = jnp.sum(rows, axis=0, keepdims=True) * norm_inv[i]
        twice = jnp.concatenate([scaled, scaled], axis=0)
        spanned = dot(jnp.concatenate(split(inner), axis=1), twice, (1, 0))
        spanned = dot(twice, jnp.concatenate(split(spanned), axis=0), (0, 0))
        gain = jnp.sqrt(rank * norm_inv[i])
        out_ref[i] = (gain * (scale * eye + norm_inv[i] * spanned) + shift).astype(BF16)


def apply_kernel(y_ref, t_ref, out_ref, *, slots, length):
    members = y_ref.shape[0]
    head = (length // 128) * 128
    tail = length - head
    low = iota((members, 128), 1) < tail
    for p in range((slots + 1) // 2):
        base = 2 * p * length
        size = 2 * length if 2 * p + 1 < slots else length
        here = pl.ds(base, size)
        states = y_ref[:, here].astype(F32)
        average = jnp.sum(states, axis=0, keepdims=True) * (1.0 / members)
        spread = (states - average).astype(BF16)
        if size == length:
            update = dot(t_ref[2 * p], spread, (1, 0))
        else:
            even = dot(t_ref[2 * p], spread[:, : head + 128], (1, 0))
            odd = dot(t_ref[2 * p + 1], spread[:, head:], (1, 0))
            update = jnp.concatenate(
                [even[:, :head], jnp.where(low, even[:, head:], odd[:, :128]), odd[:, 128:]], axis=1
            )
        out_ref[:, here] = (average + update).astype(BF16)


def exchange(blocks):
    return lax.all_to_all(blocks, "member", split_axis=0, concat_axis=0, tiled=True)


SMEM = pl.BlockSpec(memory_space=pltpu.SMEM)
VMEM = pl.BlockSpec(memory_space=pltpu.VMEM)
PARAMS = pltpu.CompilerParams(vmem_limit_bytes=48 * 2**20)


def lane_tiles(shape):
    return pltpu.VMEM((pl.cdiv(shape[1], 128), shape[0], 128), F32)


def pack(states, slots, groups):
    part_rows, length, _ = states.shape
    shape = (groups * part_rows, slots * length)
    return pl.pallas_call(
        lambda *refs: pack_kernel(*refs, slots=slots, groups=groups),
        out_shape=jax.ShapeDtypeStruct(shape, BF16),
        in_specs=[VMEM],
        out_specs=VMEM,
        scratch_shapes=[lane_tiles(shape)],
        compiler_params=PARAMS,
        name="pack",
    )(states)


def unpack(live, states, finished, slots, groups):
    return pl.pallas_call(
        lambda *refs: unpack_kernel(*refs, slots=slots, groups=groups),
        out_shape=jax.ShapeDtypeStruct(states.shape, BF16),
        in_specs=[SMEM, VMEM, VMEM],
        out_specs=VMEM,
        scratch_shapes=[lane_tiles(finished.shape)],
        compiler_params=PARAMS,
        name="unpack",
    )(live, states, finished)


def transforms(departures, innovations, precision, obs_count, slots):
    _, obs, members = departures.shape
    square = pltpu.VMEM((slots, obs, obs), F32)
    return pl.pallas_call(
        transform_kernel,
        out_shape=jax.ShapeDtypeStruct((slots, members, members), BF16),
        in_specs=[SMEM, VMEM, VMEM, VMEM],
        out_specs=VMEM,
        scratch_shapes=[
            pltpu.VMEM((slots, obs, members), BF16),
            square,
            pltpu.VMEM((slots, 4 * obs, obs), BF16),
            square,
            square,
        ],
        compiler_params=PARAMS,
        name="transform",
    )(obs_count, departures, innovations, precision)


def apply(states, transform, slots, length):
    return pl.pallas_call(
        lambda *refs: apply_kernel(*refs, slots=slots, length=length),
        out_shape=jax.ShapeDtypeStruct(states.shape, BF16),
        in_specs=[VMEM, VMEM],
        out_specs=VMEM,
        compiler_params=PARAMS,
        name="apply",
    )(states, transform)


def analyse(slots, groups, live, states, departures, innovations, precision, obs_count):
    part_rows, length, _ = states.shape
    members = groups * part_rows
    width = slots * length
    packed = pack(states, slots, groups)
    columns = exchange(packed.reshape(groups, part_rows, width)).reshape(members, width)
    transform = transforms(departures, innovations, precision, obs_count, slots)
    result = apply(columns, transform, slots, length)
    home = exchange(result.reshape(groups, part_rows, width)).reshape(members, width)
    return unpack(live, states, home, slots, groups)


def on_device(ensemble, departures, innovations, precision, obs_count, tile_counts):
    groups = lax.axis_size("member")
    capacity = departures.shape[0]
    here = jnp.arange(tile_counts.shape[0]) == lax.axis_index("tile")
    live = (jnp.sum(jnp.where(here, tile_counts, 0), keepdims=True) // groups).astype(jnp.int32)
    states = ensemble.transpose(0, 2, 1)
    result = analyse(
        capacity, groups, live, states, departures, innovations, precision, obs_count
    )
    return result.transpose(0, 2, 1)


def solution(mesh):
    placed = (
        P("member", "tile", None),
        P(("tile", "member"), None, None),
        P(("tile", "member"), None),
        P(("tile", "member"), None),
        P(("tile", "member")),
        P(),
    )
    return jax.shard_map(
        on_device, mesh=mesh, in_specs=placed, out_specs=P("member", "tile", None), check_vma=False
    )
```

profile of v0, /device:TPU:32, one launch (start us, length us, event | category | flops | bytes accessed | tf_op | source)
XLA Modules:
  0.0 64.5 jit_solution(6852666368266234674)
XLA Ops:
  0.0 0.0 copy-start
  0.0 1.1 %copy-done = bf16[8,128,320]{1,2,0:T(8,128)(2,1)S(1)} copy-done((bf16[8,128,320]{1,2,0:T(8,128)(2,1)S(1)}, bf16[8,128,320]{1,2,0:T(8,128)(2,1)}, u32[]{:S(2)}) %copy-start) | copy-done | bytes 655384
  1.1 1.7 %pack.1 = bf16[256,1280]{1,0:T(8,128)(2,1)} custom-call(bf16[8,320,128]{2,1,0:T(8,128)(2,1)S(1)} %bitcast.8), custom_call_target="tpu_custom_call" | custom-call | tf_op jit(solution)/shard_map/pack/pallas_call | solution.py:234
  2.8 0.0 copy-start.2
  2.8 0.0 copy-start.3
  2.8 0.0 copy-start.4
  2.8 0.0 copy-start.5
  2.8 13.3 %all-to-all-start = ((bf16[32,8,1280]{2,1,0:T(8,128)(2,1)}), bf16[32,8,1280]{2,1,0:T(8,128)(2,1)S(1)}, u32[]{:S(2)}, u32[]{:S(2)}) async-start(bf16[32,8,1280]{2,1,0:T(8,128)(2,1)} %bitcast.2), calls=%async_computation | async-start | bytes 1310720 | tf_op jit(solution)/shard_map/all_to_all | solution.py:219
  16.2 0.0 copy-done.2
  16.2 0.0 copy-done.3
  16.2 0.0 copy-done.4
  16.2 0.0 copy-done.5
  16.2 5.2 %transform.1.refs_1_ = bf16[4,256,256]{2,1,0:T(8,128)(2,1)S(1)} custom-call(s32[4]{0:T(128)S(1)} %copy-done.5, bf16[4,128,256]{2,1,0:T(8,128)(2,1)S(1)} %copy-done.2, f32[4,128]{1,0:T(4,128)S(1)} %copy-done.3, f32[4,128]{1,0:T(4,128)S(1)} %copy-done.4), custom_call_target="tpu_custom_call" | custom-call | tf_op jit(solution)/shard_map/transform/pallas_call | solution.py:260
  21.5 14.8 %all-to-all-done = bf16[32,8,1280]{2,1,0:T(8,128)(2,1)S(1)} async-done(((bf16[32,8,1280]{2,1,0:T(8,128)(2,1)}), bf16[32,8,1280]{2,1,0:T(8,128)(2,1)S(1)}, u32[]{:S(2)}, u32[]{:S(2)}) %all-to-all-start) | async-done | bytes 655392 | tf_op jit(solution)/shard_map/all_to_all | solution.py:219
  36.3 1.4 %apply.1 = bf16[256,1280]{1,0:T(8,128)(2,1)} custom-call(bf16[256,1280]{1,0:T(8,128)(2,1)S(1)} %bitcast.7, bf16[4,256,256]{2,1,0:T(8,128)(2,1)S(1)} %transform.1.refs_1_), custom_call_target="tpu_custom_call" | custom-call | tf_op jit(solution)/shard_map/apply/pallas_call | solution.py:278
  37.7 0.0 copy-start.1
  37.7 5.3 %all-to-all-start.1 = ((bf16[32,8,1280]{2,1,0:T(8,128)(2,1)}), bf16[32,8,1280]{2,1,0:T(8,128)(2,1)S(1)}, u32[]{:S(2)}, u32[]{:S(2)}) async-start(bf16[32,8,1280]{2,1,0:T(8,128)(2,1)} %bitcast.4), calls=%async_computation.1 | async-start | bytes 1310720 | tf_op jit(solution)/shard_map/all_to_all | solution.py:219
  43.0 0.0 copy-start.6
  43.0 0.6 %copy-done.6 = s32[16]{0:T(128)S(1)} copy-done((s32[16]{0:T(128)S(1)}, s32[16]{0:T(128)}, u32[]{:S(2)}) %copy-start.6) | copy-done | bytes 88
  43.6 0.7 %fusion = s32[]{:T(128)} fusion(s32[16]{0:T(128)S(1)} %copy-done.6, s32[]{:T(128)S(6)} %axis_index.12), kind=kLoop, calls=%fused_computation.1 | loop fusion | flops 47 | bytes 72 | tf_op jit(solution)/shard_map/reduce_sum | solution.py:304
  47.1 16.0 %all-to-all-done.1 = bf16[32,8,1280]{2,1,0:T(8,128)(2,1)S(1)} async-done(((bf16[32,8,1280]{2,1,0:T(8,128)(2,1)}), bf16[32,8,1280]{2,1,0:T(8,128)(2,1)S(1)}, u32[]{:S(2)}, u32[]{:S(2)}) %all-to-all-start.1) | async-done | bytes 655392 | tf_op jit(solution)/shard_map/all_to_all | solution.py:219
  63.0 0.0 copy-done.1
  63.0 1.5 %unpack.1 = bf16[8,320,128]{2,1,0:T(8,128)(2,1)} custom-call(s32[1]{0:T(128)S(6)} %select_n.10.refs_0_, bf16[8,320,128]{2,1,0:T(8,128)(2,1)S(1)} %bitcast.9, bf16[256,1280]{1,0:T(8,128)(2,1)S(1)} %bitcast.10), custom_call_target="tpu_custom_call" | custom-call | tf_op jit(solution)/shard_map/unpack/pallas_call | solution.py:246
Async XLA Ops:
  0.0 1.1 %copy-start = (bf16[8,128,320]{1,2,0:T(8,128)(2,1)S(1)}, bf16[8,128,320]{1,2,0:T(8,128)(2,1)}, u32[]{:S(2)}) copy-start(bf16[8,128,320]{1,2,0:T(8,128)(2,1)} %param.6) | copy-start | bytes 1966084
  2.8 13.3 %copy-start.2 = (bf16[4,128,256]{2,1,0:T(8,128)(2,1)S(1)}, bf16[4,128,256]{2,1,0:T(8,128)(2,1)}, u32[]{:S(2)}) copy-start(bf16[4,128,256]{2,1,0:T(8,128)(2,1)} %dep_ref.1) | copy-start | bytes 786436
  2.8 13.3 %copy-start.3 = (f32[4,128]{1,0:T(4,128)S(1)}, f32[4,128]{1,0:T(4,128)}, u32[]{:S(2)}) copy-start(f32[4,128]{1,0:T(4,128)} %inn_ref.1) | copy-start | bytes 6148
  2.8 13.3 %copy-start.4 = (f32[4,128]{1,0:T(4,128)S(1)}, f32[4,128]{1,0:T(4,128)}, u32[]{:S(2)}) copy-start(f32[4,128]{1,0:T(4,128)} %prec_ref.1) | copy-start | bytes 6148
  2.8 13.4 %copy-start.5 = (s32[4]{0:T(128)S(1)}, s32[4]{0:T(128)}, u32[]{:S(2)}) copy-start(s32[4]{0:T(128)} %count_ref.1) | copy-start | bytes 52
  2.8 33.5 %all-to-all-start = ((bf16[32,8,1280]{2,1,0:T(8,128)(2,1)}), bf16[32,8,1280]{2,1,0:T(8,128)(2,1)S(1)}, u32[]{:S(2)}, u32[]{:S(2)}) async-start(bf16[32,8,1280]{2,1,0:T(8,128)(2,1)} %bitcast.2), calls=%async_computation | async-start | bytes 1310720 | tf_op jit(solution)/shard_map/all_to_all | solution.py:219
  37.7 25.4 %copy-start.1 = (bf16[8,128,320]{1,2,0:T(8,128)(2,1)S(1)}, bf16[8,128,320]{1,2,0:T(8,128)(2,1)}, u32[]{:S(2)}) copy-start(bf16[8,128,320]{1,2,0:T(8,128)(2,1)} %param.6) | copy-start | bytes 1966084
  37.7 25.4 %all-to-all-start.1 = ((bf16[32,8,1280]{2,1,0:T(8,128)(2,1)}), bf16[32,8,1280]{2,1,0:T(8,128)(2,1)S(1)}, u32[]{:S(2)}, u32[]{:S(2)}) async-start(bf16[32,8,1280]{2,1,0:T(8,128)(2,1)} %bitcast.4), calls=%async_computation.1 | async-start | bytes 1310720 | tf_op jit(solution)/shard_map/all_to_all | solution.py:219
  43.0 0.7 %copy-start.6 = (s32[16]{0:T(128)S(1)}, s32[16]{0:T(128)}, u32[]{:S(2)}) copy-start(s32[16]{0:T(128)} %param.11) | copy-start | bytes 196
where the time goes:
time: 64.9 us; the launch traced here: 64.5 us
  waiting for transfers between devices  30.8 us (47%)
  starting transfers between devices  18.6 us (29%)
  Pallas kernels  9.84 us (15%)
  between operations  2.82 us (4%)
  local copies, waits for them, and re-layouts  1.76 us (3%)
  other arithmetic  0.7 us (1%)
    all_to_all x2, waiting for transfers between devices, exchange(): lax.all_to_all(blocks, 'member', split_axis=0, concat_axis=0, tiled=True)  30.8 us
    all_to_all x2, starting transfers between devices, exchange(): lax.all_to_all(blocks, 'member', split_axis=0, concat_axis=0, tiled=True)  18.6 us
    pallas_call x1, Pallas kernels, transforms(): pl.pallas_call(transform_kernel, out_shape=jax.ShapeDtypeStruct((slots, m...  5.25 us
    unnamed x14, local copies, waits for them, and re-layouts  1.76 us
    pallas_call x1, Pallas kernels, pack(): pl.pallas_call(lambda *refs: pack_kernel(*refs, slots=slots, groups=group...  1.74 us
    pallas_call x1, Pallas kernels, unpack(): pl.pallas_call(lambda *refs: unpack_kernel(*refs, slots=slots, groups=gro...  1.49 us
    pallas_call x1, Pallas kernels, apply(): pl.pallas_call(lambda *refs: apply_kernel(*refs, slots=slots, length=leng...  1.36 us
  transfers between devices with their start and end apart: 2, of which 2 were waited for; matrix products, arithmetic and copies ran while one was open for 1% of the time, Pallas kernels for 8%

commit v1 on v0

--- a/solution.py
+++ b/solution.py
@@ -285,16 +285,19 @@
     )(states, transform)
 
 
-def analyse(slots, groups, live, states, departures, innovations, precision, obs_count):
-    part_rows, length, _ = states.shape
-    members = groups * part_rows
-    width = slots * length
-    packed = pack(states, slots, groups)
-    columns = exchange(packed.reshape(groups, part_rows, width)).reshape(members, width)
-    transform = transforms(departures, innovations, precision, obs_count, slots)
-    result = apply(columns, transform, slots, length)
-    home = exchange(result.reshape(groups, part_rows, width)).reshape(members, width)
-    return unpack(live, states, home, slots, groups)
+def with_slots(slots, groups):
+    def run(live, states, packed, departures, innovations, precision, obs_count):
+        part_rows, length, _ = states.shape
+        members = groups * part_rows
+        width = slots * length
+        sent = packed[:, :width].reshape(groups, part_rows, width)
+        columns = exchange(sent).reshape(members, width)
+        transform = transforms(departures, innovations, precision, obs_count, slots)
+        result = apply(columns, transform, slots, length)
+        home = exchange(result.reshape(groups, part_rows, width)).reshape(members, width)
+        return unpack(live, states, home, slots, groups)
+
+    return run
 
 
 def on_device(ensemble, departures, innovations, precision, obs_count, tile_counts):
@@ -303,8 +306,18 @@
     here = jnp.arange(tile_counts.shape[0]) == lax.axis_index("tile")
     live = (jnp.sum(jnp.where(here, tile_counts, 0), keepdims=True) // groups).astype(jnp.int32)
     states = ensemble.transpose(0, 2, 1)
-    result = analyse(
-        capacity, groups, live, states, departures, innovations, precision, obs_count
+    packed = pack(states, capacity, groups)
+    fewest = 2
+    result = lax.switch(
+        jnp.clip(live[0], fewest, capacity) - fewest,
+        [with_slots(slots, groups) for slots in range(fewest, capacity + 1)],
+        live,
+        states,
+        packed,
+        departures,
+        innovations,
+        precision,
+        obs_count,
     )
     return result.transpose(0, 2, 1)
 

time: 64.9 us -> 60.4 us (0.931)
  the two profiles are of different devices: /device:TPU:32 before, /device:TPU:40 now
where the time goes in v1:
time: 60.4 us; the launch traced here: 59.2 us
  blocking collectives  21.3 us (35%)
  starting transfers between devices  13.2 us (22%)
  waiting for transfers between devices  9.84 us (16%)
  Pallas kernels  8.34 us (14%)
  local copies, waits for them, and re-layouts  3.24 us (5%)
  between operations  2.69 us (4%)
  other arithmetic  0.63 us (1%)
    all_to_all x1, blocking collectives, exchange(): lax.all_to_all(blocks, 'member', split_axis=0, concat_axis=0, tiled=True)  21.3 us
    all_to_all x1, starting transfers between devices, exchange(): lax.all_to_all(blocks, 'member', split_axis=0, concat_axis=0, tiled=True)  13.2 us
    all_to_all x1, waiting for transfers between devices, exchange(): lax.all_to_all(blocks, 'member', split_axis=0, concat_axis=0, tiled=True)  9.84 us
    pallas_call x1, Pallas kernels, transforms(): pl.pallas_call(transform_kernel, out_shape=jax.ShapeDtypeStruct((slots, m...  4.48 us
    pallas_call x1, Pallas kernels, pack(): pl.pallas_call(lambda *refs: pack_kernel(*refs, slots=slots, groups=group...  2.9 us
    reshape x1, local copies, waits for them, and re-layouts, run(): sent = packed[:, :width].reshape(groups, part_rows, width)  1.72 us
    unnamed x14, local copies, waits for them, and re-layouts  1.52 us
  transfers between devices with their start and end apart: 1, of which 1 were waited for; matrix products, arithmetic and copies ran while one was open for 0% of the time, Pallas kernels for 8%

profile of v1, /device:TPU:40, one launch (start us, length us, event | category | flops | bytes accessed | tf_op | source)
XLA Modules:
  0.0 59.2 jit_solution(9577252208564086386)
XLA Ops:
  0.0 0.0 copy-start.6
  0.0 0.7 %copy-done.6 = s32[16]{0:T(128)S(1)} copy-done((s32[16]{0:T(128)S(1)}, s32[16]{0:T(128)}, u32[]{:S(2)}) %copy-start.6) | copy-done | bytes 88
  0.7 0.6 %fusion = s32[]{:T(128)} fusion(s32[16]{0:T(128)S(1)} %copy-done.6, s32[]{:T(128)S(6)} %axis_index.12), kind=kLoop, calls=%fused_computation.3 | loop fusion | flops 47 | bytes 72 | tf_op jit(solution)/shard_map/reduce_sum | solution.py:307
  3.9 0.0 copy-start
  3.9 0.0 copy-start.1
  3.9 0.0 copy-start.3
  3.9 0.0 copy-start.4
  3.9 0.0 copy-start.5
  4.0 2.9 %pack.1 = bf16[256,1280]{1,0:T(8,128)(2,1)} custom-call(bf16[8,320,128]{2,1,0:T(8,128)(2,1)} %bitcast.27), custom_call_target="tpu_custom_call" | custom-call | tf_op jit(solution)/shard_map/pack/pallas_call | solution.py:234
  6.9 0.0 copy-done
  6.9 0.0 copy-done.1
  6.9 0.0 copy-done.3
  6.9 0.0 copy-done.4
  6.9 0.0 copy-done.5
  6.9 51.5 %conditional.1 = (bf16[8,320,128]{2,1,0:T(8,128)(2,1)S(1)}) conditional(s32[]{:T(128)} %bitcast.13, (bf16[256,1280]{1,0:T(8,128)(2,1)}, s32[4]{0:T(128)S(1)}, bf16[4,128,256]{2,1,0:T(8,128)(2,1)S(1)}, f32[4,128]{1,0:T(4,128)S(1)}, f32[4,128]{1,0:T(4,128)S(1)}, /*index=5*/s32[1]{0:T(128)}, ...), branch_computations={%region_1.2_spmd, %region_2.3_spmd, %region_3.4_spmd} | conditional | bytes 3506216 | solution.py:311
  6.9 1.7 %slice_bitcast_fusion = bf16[32,8,640]{2,1,0:T(8,128)(2,1)} fusion(bf16[256,1280]{1,0:T(8,128)(2,1)} %get-tuple-element.53), kind=kLoop, calls=%fused_computation | loop fusion | bytes 655360 | tf_op jit(solution)/shard_map/cond/branch_0_fun/reshape | solution.py:293
  8.6 13.2 %all-to-all-start.2 = ((bf16[32,8,640]{2,1,0:T(8,128)(2,1)}), bf16[32,8,640]{2,1,0:T(8,128)(2,1)S(1)}, u32[]{:S(2)}, u32[]{:S(2)}) async-start(bf16[32,8,640]{2,1,0:T(8,128)(2,1)} %slice_bitcast_fusion), calls=%async_computation.2 | async-start | bytes 655360 | tf_op jit(solution)/shard_map/cond/branch_0_fun/all_to_all | solution.py:219
  21.8 4.5 %transform.3.refs_1_ = bf16[2,256,256]{2,1,0:T(8,128)(2,1)S(1)} custom-call(s32[4]{0:T(128)S(1)} %get-tuple-element.54.count_ref, bf16[4,128,256]{2,1,0:T(8,128)(2,1)S(1)} %get-tuple-element.55.dep_ref, f32[4,128]{1,0:T(4,128)S(1)} %get-tuple-element.56.inn_ref, f32[4,128]{1,0:T(4,128)S(1)} %get-tuple-element.57.prec_ref), custom_call_target="tpu_custom_call" | custom-call | tf_op jit(solution)/shard_map/cond/branch_0_fun/transform/pallas_call | solution.py:260
  26.3 9.8 %all-to-all-done.2 = bf16[32,8,640]{2,1,0:T(8,128)(2,1)S(1)} async-done(((bf16[32,8,640]{2,1,0:T(8,128)(2,1)}), bf16[32,8,640]{2,1,0:T(8,128)(2,1)S(1)}, u32[]{:S(2)}, u32[]{:S(2)}) %all-to-all-start.2) | async-done | bytes 327712 | tf_op jit(solution)/shard_map/cond/branch_0_fun/all_to_all | solution.py:219
  36.1 0.4 apply.3
  36.5 21.3 %all_to_all.24 = bf16[32,8,640]{2,1,0:T(8,128)(2,1)S(1)} all-to-all(bf16[32,8,640]{2,1,0:T(8,128)(2,1)S(1)} %bitcast.25), channel_id=1, replica_groups=mesh['member'=32,'tile'=16] {'member'}, dimensions={0} | all-to-all | bytes 655360 | tf_op jit(solution)/shard_map/cond/branch_0_fun/all_to_all | solution.py:219
  57.8 0.6 %unpack.3 = bf16[8,320,128]{2,1,0:T(8,128)(2,1)S(1)} custom-call(s32[1]{0:T(128)} %get-tuple-element.50.refs_0_, bf16[8,320,128]{2,1,0:T(8,128)(2,1)S(1)} %get-tuple-element.52.refs_1_, bf16[256,640]{1,0:T(8,128)(2,1)S(1)} %bitcast.26), custom_call_target="tpu_custom_call" | custom-call | tf_op jit(solution)/shard_map/cond/branch_0_fun/unpack/pallas_call | solution.py:246
  58.4 0.0 copy-start.2
  58.4 0.8 %copy-done.2 = bf16[8,320,128]{2,1,0:T(8,128)(2,1)} copy-done((bf16[8,320,128]{2,1,0:T(8,128)(2,1)}, bf16[8,320,128]{2,1,0:T(8,128)(2,1)S(1)}, u32[]{:S(2)}) %copy-start.2) | copy-done | bytes 655384
Async XLA Ops:
  0.0 0.7 %copy-start.6 = (s32[16]{0:T(128)S(1)}, s32[16]{0:T(128)}, u32[]{:S(2)}) copy-start(s32[16]{0:T(128)} %param.14) | copy-start | bytes 196
  3.9 3.0 %copy-start = (bf16[8,128,320]{1,2,0:T(8,128)(2,1)S(1)}, bf16[8,128,320]{1,2,0:T(8,128)(2,1)}, u32[]{:S(2)}) copy-start(bf16[8,128,320]{1,2,0:T(8,128)(2,1)} %param.9) | copy-start | bytes 1966084
  3.9 3.0 %copy-start.1 = (bf16[4,128,256]{2,1,0:T(8,128)(2,1)S(1)}, bf16[4,128,256]{2,1,0:T(8,128)(2,1)}, u32[]{:S(2)}) copy-start(bf16[4,128,256]{2,1,0:T(8,128)(2,1)} %param.10) | copy-start | bytes 786436
  3.9 2.9 %copy-start.3 = (f32[4,128]{1,0:T(4,128)S(1)}, f32[4,128]{1,0:T(4,128)}, u32[]{:S(2)}) copy-start(f32[4,128]{1,0:T(4,128)} %param.11) | copy-start | bytes 6148
  3.9 2.9 %copy-start.4 = (f32[4,128]{1,0:T(4,128)S(1)}, f32[4,128]{1,0:T(4,128)}, u32[]{:S(2)}) copy-start(f32[4,128]{1,0:T(4,128)} %param.12) | copy-start | bytes 6148
  3.9 2.9 %copy-start.5 = (s32[4]{0:T(128)S(1)}, s32[4]{0:T(128)}, u32[]{:S(2)}) copy-start(s32[4]{0:T(128)} %param.13) | copy-start | bytes 52
  8.6 27.5 %all-to-all-start.2 = ((bf16[32,8,640]{2,1,0:T(8,128)(2,1)}), bf16[32,8,640]{2,1,0:T(8,128)(2,1)S(1)}, u32[]{:S(2)}, u32[]{:S(2)}) async-start(bf16[32,8,640]{2,1,0:T(8,128)(2,1)} %slice_bitcast_fusion), calls=%async_computation.2 | async-start | bytes 655360 | tf_op jit(solution)/shard_map/cond/branch_0_fun/all_to_all | solution.py:219
  58.4 0.8 %copy-start.2 = (bf16[8,320,128]{2,1,0:T(8,128)(2,1)}, bf16[8,320,128]{2,1,0:T(8,128)(2,1)S(1)}, u32[]{:S(2)}) copy-start(bf16[8,320,128]{2,1,0:T(8,128)(2,1)S(1)} %get-tuple-element.72) | copy-start | bytes 1966084
